TPU v7x, 128 devices: a whole 4x4x4 slice. The times are simulated.
128 devices in a mesh: layer: 4 (over z_hi, core), row: 32 (over x, y, z_lo).
Axes of the slice: x: 4, y: 4, z: 4 (z_hi: 2, z_lo: 2; z = z_hi * 2 + z_lo), core: 2. Of those that a mesh axis runs over, the one named last changes fastest.
Arguments:
- magnet: float32 [3, 4, 2048, 2048], P(None, 'layer', 'row'), may hold values from -6 to 6
- kernel: float32 [7, 6, 2048, 2048], P(None, None, ('layer', 'row')), may hold values from -1.8 to 1.8, as said below
Outputs:
- demag: float32 [3, 4, 2048, 2048], P(None, 'layer', 'row')
Inputs may be any that keep to these rules, and one draw needn't show every extreme that they name: With q' = -q mod 2048 and p' = -p mod 2048: parts 0, 1, 2 satisfy kernel[o, j, q', p] = kernel[o, j, q, p'] = kernel[o, j, q, p]; part 3 changes sign under either mirror; part 4 changes sign under p -> p' and keeps it under q -> q'; part 5 keeps its sign under p -> p' and changes it under q -> q'.
All inputs are finite; a program needn't handle non-finite values.
Results may differ from a plain program's by a relative error of at most 0.0001.
Values sent between devices are 32-bit elements; how exact they have to be, the bound alone decides.
No kernel may reach another device: no remote copies, remote signals or barrier semaphores. Data moves between devices by JAX's collectives and lax.ppermute only.
A program may use at most 256 MiB of HBM per device.

v0:
```python
import math

import jax
import jax.numpy as jnp
import numpy as np
from jax import lax
from jax.experimental import pallas as pl
from jax.experimental.pallas import tpu as pltpu
from jax.sharding import PartitionSpec as P


CELLS = 2048
COMPS = 3
LAYERS = 4
ROWS = 32
X_ROWS = 64
DEVICES = 128
PARTS = 6
OFFSETS = 7
OPS = OFFSETS * PARTS
FINE = 128
COARSE = 16
OWNED = 8
SLOT = COMPS * OWNED
LANES = 128
EXTRA = 16
P1_ROWS = LAYERS * COMPS * OWNED
P1_ALL = P1_ROWS + EXTRA

F32 = jnp.float32
BF16 = jnp.bfloat16


def halves(table):
    high = np.asarray(table, np.float32).astype(jnp.bfloat16)
    low = (np.asarray(table, np.float64) - high.astype(np.float64)).astype(np.float32).astype(jnp.bfloat16)
    return high, low


def fine_table():
    index = np.arange(FINE)
    angle = 2.0 * np.pi * (np.outer(index, index) % FINE) / FINE
    return np.block([[np.cos(angle), -np.sin(angle)], [np.sin(angle), np.cos(angle)]])


def stacked(table):
    return np.concatenate(halves(table), axis=0)


def y_twiddle(sign, scale):
    k = np.arange(1, COARSE // 2 + 1)[:, None]
    b = np.arange(FINE)[None, :]
    angle = 2.0 * np.pi * k * b / CELLS
    table = scale * np.stack([np.cos(angle), sign * np.sin(angle)], axis=1)
    return table.reshape(COARSE, FINE).astype(np.float32)


def x_twiddle(sign, scale, inner):
    k = np.arange(ROWS // 2 + 1)[:, None]
    t = np.arange(X_ROWS)[None, :]
    angle = 2.0 * np.pi * k * t / CELLS
    cosine = scale * np.cos(angle)
    sine = scale * sign * np.sin(angle)
    lines = [
        np.concatenate([cosine, cosine], axis=1),
        np.concatenate([sine, sine], axis=1),
        np.concatenate([inner * sine, -inner * sine], axis=1),
        np.concatenate([inner * cosine, -inner * cosine], axis=1),
    ]
    return np.stack(lines, axis=1).astype(np.float32).reshape(-1, LANES)


def x_table(sign, shift):
    index = np.arange(X_ROWS)
    place = np.outer(index, index + shift) if sign < 0 else np.outer(index + shift, index)
    angle = 2.0 * np.pi * (place % X_ROWS) / X_ROWS
    real = np.cos(angle)
    imag = sign * np.sin(angle)
    whole = np.block([[real, imag], [-imag, real]])
    high, low = halves(whole)
    line = np.concatenate([high, low], axis=1)
    return np.concatenate([line, line], axis=0)


def x_tables(sign):
    return np.concatenate([x_table(sign, 0), x_table(sign, 1)], axis=0)


def real_dft(values):
    n = len(values)
    if n == 1:
        return [values[0]], [None]
    if n == 2:
        return [values[0] + values[1], values[0] - values[1]], [None, None]
    even_c, even_s = real_dft(values[0::2])
    odd_c, odd_s = real_dft(values[1::2])
    half = n // 2
    quarter = n // 4
    cos_out = [None] * (half + 1)
    sin_out = [None] * (half + 1)
    for k in range(quarter + 1):
        if k == 0:
            cos_out[0] = even_c[0] + odd_c[0]
            cos_out[half] = even_c[0] - odd_c[0]
        elif k == quarter:
            cos_out[k] = even_c[k]
            sin_out[k] = odd_c[k]
        else:
            theta = 2.0 * math.pi * k / n
            cosine, sine = math.cos(theta), math.sin(theta)
            if 8 * k == n:
                real = cosine * (odd_c[k] - odd_s[k])
                imag = cosine * (odd_s[k] + odd_c[k])
            else:
                real = cosine * odd_c[k] - sine * odd_s[k]
                imag = cosine * odd_s[k] + sine * odd_c[k]
            cos_out[k] = even_c[k] + real
            sin_out[k] = even_s[k] + imag
            cos_out[half - k] = even_c[k] - real
            sin_out[half - k] = imag - even_s[k]
    return cos_out, sin_out


def real_sum(cos_in, sin_in, n):
    if n == 1:
        return [cos_in[0]]
    half = n // 2
    if n == 2:
        return [cos_in[0] + cos_in[1], cos_in[0] - cos_in[1]]
    quarter = n // 4
    even_c = [None] * (quarter + 1)
    even_s = [None] * (quarter + 1)
    odd_c = [None] * (quarter + 1)
    odd_s = [None] * (quarter + 1)
    even_c[0] = cos_in[0] + cos_in[half]
    odd_c[0] = cos_in[0] - cos_in[half]
    even_c[quarter] = cos_in[quarter]
    odd_c[quarter] = sin_in[quarter]
    for k in range(1, quarter):
        theta = 2.0 * math.pi * k / n
        cosine, sine = math.cos(theta), math.sin(theta)
        even_c[k] = cos_in[k] + cos_in[half - k]
        even_s[k] = sin_in[k] - sin_in[half - k]
        gap = cos_in[k] - cos_in[half - k]
        both = sin_in[k] + sin_in[half - k]
        if 8 * k == n:
            odd_c[k] = cosine * (gap + both)
            odd_s[k] = cosine * (both - gap)
        else:
            odd_c[k] = cosine * gap + sine * both
            odd_s[k] = cosine * both - sine * gap
    evens = real_sum(even_c, even_s, half)
    odds = real_sum(odd_c, odd_s, half)
    out = [None] * n
    out[0::2] = evens
    out[1::2] = odds
    return out


def split_pair(value):
    high = value.astype(BF16)
    low = (value - high.astype(F32)).astype(BF16)
    return high, low


def dot(left, right):
    return jnp.dot(left, right, preferred_element_type=F32)


def triple_dot(high, low, table_ref):
    size = table_ref.shape[0] // 2
    table_high, table_low = table_ref[:size, :], table_ref[size:, :]
    left = jnp.concatenate([high, low, high], axis=1)
    return dot(left, jnp.concatenate([table_high, table_high, table_low], axis=0))


def slot_rows(comp, k1):
    half = DEVICES // 2
    near = pl.ds(comp * OWNED + k1, half, stride=SLOT)
    far = pl.ds(half * SLOT + comp * OWNED + k1 - 1, half, stride=SLOT)
    return near, far


EDGE_PARTS = 4
EDGES = OFFSETS * EDGE_PARTS


def edge_kernel(kernel_hbm, out_ref, tiles_ref, sem):
    n_tiles = CELLS // LANES
    copies = []
    for j in range(n_tiles):
        lanes = pl.ds(LANES * j, LANES)
        for i, (source, target) in enumerate([((0, 3), (0, 3)), ((4, 1), (3, 1))]):
            copy = pltpu.make_async_copy(
                kernel_hbm.at[:, pl.ds(*source), pl.ds(0, 1), lanes],
                tiles_ref.at[j, :, pl.ds(*target)],
                sem.at[j, i],
            )
            copy.start()
            copies.append(copy)
    flat = tiles_ref.reshape(n_tiles * EDGES, LANES)
    for j in range(n_tiles):
        copies[2 * j].wait()
        copies[2 * j + 1].wait()
        out_ref[:, LANES * j : LANES * (j + 1)] = flat[pl.ds(j * EDGES, EDGES), :]


def forward_y_kernel(x_ref, table_ref, twiddle_ref, out_hbm, high_ref, low_ref, out_ref, sem):
    slots = out_ref.reshape(DEVICES, SLOT, LANES)
    saves = []
    edges = []
    half = DEVICES // 2
    middle = COARSE // 2
    group = 16
    lane = lax.broadcasted_iota(jnp.int32, (X_ROWS, LANES), 1)
    alternate = 1.0 - 2.0 * (lax.broadcasted_iota(jnp.int32, (X_ROWS, FINE), 1) % 2).astype(F32)
    for comp in range(COMPS):
        base = comp * (middle + 1) * X_ROWS
        nyquist = []
        for g in range(X_ROWS // group):
            top = comp * X_ROWS + g * group
            parts = [x_ref[top : top + group, FINE * a : FINE * (a + 1)] for a in range(COARSE)]
            cos_out, sin_out = real_dft(parts)
            nyquist.append(jnp.sum(cos_out[0] * alternate[:group], axis=1, keepdims=True))
            for k in range(middle + 1):
                rows = slice(base + k * X_ROWS + g * group, base + k * X_ROWS + (g + 1) * group)
                real = cos_out[k]
                imag = None
                if k > 0:
                    cosine = twiddle_ref[2 * k - 2 : 2 * k - 1, :]
                    sine = twiddle_ref[2 * k - 1 : 2 * k, :]
                    if k == middle:
                        real, imag = real * cosine, real * sine
                    else:
                        real, imag = real * cosine + sin_out[k] * sine, real * sine - sin_out[k] * cosine
                high_ref[rows, :LANES], low_ref[rows, :LANES] = split_pair(real)
                if imag is None:
                    zero = jnp.zeros((group, LANES), BF16)
                    high_ref[rows, LANES:], low_ref[rows, LANES:] = zero, zero
                else:
                    high_ref[rows, LANES:], low_ref[rows, LANES:] = split_pair(imag)
        edges.append(jnp.concatenate(nyquist, axis=0))
    out = triple_dot(high_ref[...], low_ref[...], table_ref)
    for comp in range(COMPS):

        def pick(k):
            row = (comp * (middle + 1) + k) * X_ROWS
            rows = out[row : row + X_ROWS]
            return rows[:, :LANES], rows[:, LANES:]

        for k in range(middle):
            real, imag = pick(k)
            if k == 0:
                last_real, last_imag = pick(middle)
                imag = jnp.where(lane == 0, edges[comp], imag)
                real = jnp.where(lane < half, real, last_real)
                imag = jnp.where(lane < half, imag, last_imag)
            if comp == COMPS - 1:
                real, imag = -imag, real
            block = jnp.concatenate([real, imag], axis=0).T
            near, far = slot_rows(comp, k)
            if k == 0:
                far = slot_rows(comp, middle)[1]
            out_ref[near, :] = block[:half]
            out_ref[far, :] = block[half:]
        lines = (slice(None), pl.ds(comp * OWNED, OWNED))
        save = pltpu.make_async_copy(slots.at[lines], out_hbm.at[lines], sem.at[comp])
        save.start()
        saves.append(save)
    for save in saves:
        save.wait()


def relayout_kernel(flag_ref, kernel_ref, out_ref, rows_ref, columns_ref):
    shifted = flag_ref[0] > 0
    n_ops = kernel_ref.shape[0] // 16
    sub = lax.broadcasted_iota(jnp.int32, (OWNED, CELLS), 0)
    for op in range(n_ops):
        low = kernel_ref[16 * op : 16 * op + 8, :]
        high = kernel_ref[16 * op + 8 : 16 * op + 16, :]
        moved = jnp.where(sub < 7, pltpu.roll(low, 7, 0), pltpu.roll(high, 7, 0))
        rows_ref[8 * op : 8 * op + 8, :] = jnp.where(shifted, moved, low)
    for tile in range(CELLS // LANES):
        block = rows_ref[:, LANES * tile : LANES * (tile + 1)].T
        columns_ref[LANES * tile : LANES * (tile + 1), : 8 * n_ops] = block

    def step(p1, carry):
        column = columns_ref[pl.ds(p1, X_ROWS, stride=ROWS), :]
        both = jnp.concatenate([column, column], axis=0).T
        out_ref[p1] = both[: 8 * n_ops]
        return carry

    lax.fori_loop(0, ROWS, step, 0, unroll=4)


def spectral_kernel(
    x_ref,
    kernel_hbm,
    delta_ref,
    twiddle_ref,
    back_twiddle_ref,
    table_ref,
    back_table_ref,
    out_ref,
    kernel_ref,
    extra_ref,
    sums_ref,
    pair_ref,
    spec_ref,
    fix_ref,
    back_ref,
    kernel_sem,
):
    fetch = pltpu.make_async_copy(kernel_hbm, kernel_ref, kernel_sem)
    fetch.start()
    half = ROWS // 2
    lane = lax.broadcasted_iota(jnp.int32, (ROWS, LANES), 1)

    extra_ref[...] = jnp.zeros_like(extra_ref)
    for layer in range(LAYERS):
        for comp in range(COMPS):
            line = x_ref[pl.ds(layer * ROWS * SLOT + comp * OWNED, ROWS, stride=SLOT), :]
            extra_ref[pl.ds(comp * LAYERS + layer, ROWS, stride=EXTRA), :] = jnp.where((lane < X_ROWS) == (comp == COMPS - 1), line, 0.0)
    fix_ref[...] = jnp.zeros_like(fix_ref)

    def store_sums(values, place):
        cos_out, sin_out = real_dft(values)
        for k in range(half + 1):
            sums_ref[pl.ds(k * P1_ALL + place, OWNED), :] = cos_out[k]
        for k in range(1, half):
            sums_ref[pl.ds((half + k) * P1_ALL + place, OWNED), :] = sin_out[k]

    def over_rows(index, carry):
        layer = index // COMPS
        comp = index % COMPS
        base = layer * (ROWS * SLOT) + comp * OWNED
        base = pl.multiple_of(base, OWNED)
        values = [x_ref[pl.ds(base + r * SLOT, OWNED), :] for r in range(ROWS)]
        store_sums(values, pl.multiple_of(index * OWNED, OWNED))
        return carry

    lax.fori_loop(0, LAYERS * COMPS, over_rows, 0)
    for group in range(2):
        values = [extra_ref[r * EXTRA + group * 8 : r * EXTRA + group * 8 + 8, :] for r in range(ROWS)]
        store_sums(values, P1_ROWS + group * 8)

    def factors(ref, k):
        return [ref[pl.ds(4 * k + j, 1), :] for j in range(4)]

    def save_pair(row, value):
        high, low = split_pair(value)
        pair_ref[pl.ds(row, value.shape[0]), :LANES] = high
        pair_ref[pl.ds(row, value.shape[0]), LANES:] = low

    n_blocks = P1_ALL // OWNED

    def blocks(ref, row, count):
        return [ref[pl.ds(row + OWNED * j, OWNED), :] for j in range(count)]

    def save_line(p1, values):
        for j in range(0, n_blocks, 2):
            save_pair(p1 * P1_ALL + OWNED * j, jnp.concatenate(values[j : j + 2], axis=0))

    def twist(k):
        f = factors(twiddle_ref, k)
        cos_rows = blocks(sums_ref, k * P1_ALL, n_blocks)
        if k in (0, half):
            even = [c * f[0] for c in cos_rows]
            odd = [c * f[2] for c in cos_rows]
        else:
            sin_rows = blocks(sums_ref, (half + k) * P1_ALL, n_blocks)
            even = [c * f[0] + v * f[1] for c, v in zip(cos_rows, sin_rows)]
            odd = [c * f[2] - v * f[3] for c, v in zip(cos_rows, sin_rows)]
        if k == 0:
            save_line(0, even)
            return
        odd = [pltpu.roll(v, X_ROWS, 1) for v in odd]
        if k != half:
            save_line(k, [a + b for a, b in zip(even, odd)])
        save_line(ROWS - k, [a - b for a, b in zip(even, odd)])

    size = 2 * LANES

    def forward_dot(first, count, which):
        rows = pl.ds(first * P1_ALL, count * P1_ALL)
        both = dot(pair_ref[rows, :], table_ref[which * size : (which + 1) * size, :])
        spec_ref[rows, :] = both[:, :LANES] + both[:, LANES:]

    for k in range(6):
        twist(k)
    forward_dot(0, 6, 0)
    forward_dot(27, 5, 1)
    for k in range(6, 11):
        twist(k)
    forward_dot(6, 5, 0)
    forward_dot(22, 5, 1)
    for k in range(11, half + 1):
        twist(k)
    forward_dot(11, 5, 0)
    forward_dot(half, 6, 1)
    fetch.wait()

    def mix(spectra, coefficient, edge=False):
        fields = []
        for target in range(LAYERS):
            total = [None, None, None]

            def add(comp, term):
                total[comp] = term if total[comp] is None else total[comp] + term

            for source in range(LAYERS):
                offset = target - source + LAYERS - 1
                mx, my, mz = spectra[source]
                if edge:
                    k = [coefficient(offset * EDGE_PARTS + j) for j in range(EDGE_PARTS)]
                    add(0, k[0] * mx + k[3] * mz)
                    add(1, k[1] * my)
                    add(2, k[3] * mx - k[2] * mz)
                    continue
                k = [coefficient(offset * PARTS + j) for j in range(PARTS)]
                add(0, k[0] * mx + k[3] * my + k[4] * mz)
                add(1, k[3] * mx + k[1] * my + k[5] * mz)
                add(2, k[4] * mx + k[5] * my - k[2] * mz)
            fields.append(total)
        return fields

    def fix_step(group, carry):
        base = group * OWNED
        spectra = [
            [
                spec_ref[pl.ds(base * P1_ALL + P1_ROWS + comp * LAYERS + source, OWNED, stride=P1_ALL), :]
                for comp in range(COMPS)
            ]
            for source in range(LAYERS)
        ]

        def coefficient(op):
            return delta_ref[pl.ds(pl.multiple_of(op * ROWS + base, OWNED), OWNED), :]

        fields = mix(spectra, coefficient, edge=True)
        for target in range(LAYERS):
            for comp in range(COMPS):
                row = base * P1_ROWS + (target * COMPS + comp) * OWNED
                fix_ref[pl.ds(row, OWNED, stride=P1_ROWS), :] = fields[target][comp]
        return carry

    lax.fori_loop(0, ROWS // OWNED, fix_step, 0)

    def mix_line(p1):
        lines = blocks(spec_ref, p1 * P1_ALL, LAYERS * COMPS)
        spectra = [lines[COMPS * s : COMPS * s + COMPS] for s in range(LAYERS)]
        kernel_base = p1 * (OPS * OWNED)

        def coefficient(op):
            return kernel_ref[pl.ds(kernel_base + op * OWNED, OWNED), :]

        fields = mix(spectra, coefficient)
        flat = [fields[j // COMPS][j % COMPS] for j in range(LAYERS * COMPS)]
        row = p1 * P1_ROWS
        fixes = blocks(fix_ref, row, LAYERS * COMPS)
        flat = [a + b for a, b in zip(flat, fixes)]
        for j in range(0, LAYERS * COMPS, 2):
            save_pair(row + OWNED * j, jnp.concatenate(flat[j : j + 2], axis=0))

    def backward_dot(p1, rows):
        which = p1 // half
        base = which * size if isinstance(p1, int) else pl.multiple_of(which * size, size)
        both = dot(pair_ref[pl.ds(p1 * P1_ROWS, rows), :], back_table_ref[pl.ds(base, size), :])
        back_ref[pl.ds(p1 * P1_ROWS, rows), :] = both[:, :LANES] + both[:, LANES:]

    span = 8
    for p1 in range(span):
        mix_line(p1)

    def mix_step(step, carry):
        p1 = pl.multiple_of(span * step, span)
        backward_dot(p1 - span, span * P1_ROWS)
        for i in range(span):
            mix_line(p1 + i)
        return carry

    lax.fori_loop(1, ROWS // span, mix_step, 0)
    backward_dot(ROWS - span, span * P1_ROWS)

    count = LAYERS * COMPS
    f = factors(back_twiddle_ref, 0)
    for j, value in enumerate(blocks(back_ref, 0, count)):
        sums_ref[pl.ds(OWNED * j, OWNED), :] = value * f[0]
    f = factors(back_twiddle_ref, half)
    for j, value in enumerate(blocks(back_ref, half * P1_ROWS, count)):
        swap = pltpu.roll(value, X_ROWS, 1)
        sums_ref[pl.ds(half * P1_ROWS + OWNED * j, OWNED), :] = value * f[0] - swap * f[2]

    def untwist(k):
        f = factors(back_twiddle_ref, k)
        near = blocks(back_ref, k * P1_ROWS, count)
        far = blocks(back_ref, (ROWS - k) * P1_ROWS, count)
        swaps = [pltpu.roll(a - b, X_ROWS, 1) for a, b in zip(near, far)]
        for j in range(count):
            plus = near[j] + far[j]
            sums_ref[pl.ds(k * P1_ROWS + OWNED * j, OWNED), :] = plus * f[0] + swaps[j] * f[2]
            sums_ref[pl.ds((half + k) * P1_ROWS + OWNED * j, OWNED), :] = swaps[j] * f[3] - plus * f[1]

    for k in range(1, half):
        untwist(k)

    def back_rows(index, carry):
        place = pl.multiple_of(index * OWNED, OWNED)
        cos_in = [sums_ref[pl.ds(k * P1_ROWS + place, OWNED), :] for k in range(half + 1)]
        sin_in = [None] + [sums_ref[pl.ds((half + k) * P1_ROWS + place, OWNED), :] for k in range(1, half)] + [None]
        values = real_sum(cos_in, sin_in, ROWS)
        layer = index // COMPS
        comp = index % COMPS
        base = pl.multiple_of(layer * (ROWS * SLOT) + comp * OWNED, OWNED)
        for r in range(ROWS):
            out_ref[pl.ds(base + r * SLOT, OWNED), :] = values[r]
        return carry

    lax.fori_loop(0, LAYERS * COMPS, back_rows, 0)


def inverse_y_kernel(x_ref, table_ref, twiddle_ref, out_hbm, high_ref, low_ref, lines_ref, result_ref, sem):
    half = DEVICES // 2
    middle = COARSE // 2
    group = 8
    lane = lax.broadcasted_iota(jnp.int32, (X_ROWS, LANES), 1)
    alternate = 1.0 - 2.0 * (lax.broadcasted_iota(jnp.int32, (group, FINE), 1) % 2).astype(F32)
    copies = []
    columns = []
    for comp in range(COMPS):
        size = (middle + 1) * X_ROWS
        base = comp * size

        def put(k, real, imag):
            rows = slice(base + k * X_ROWS, base + (k + 1) * X_ROWS)
            high_ref[rows, :LANES], low_ref[rows, :LANES] = split_pair(real)
            high_ref[rows, LANES:], low_ref[rows, LANES:] = split_pair(imag)

        for k in range(middle):
            near, far = slot_rows(comp, k)
            if k == 0:
                far = slot_rows(comp, middle)[1]
            block = jnp.concatenate([x_ref[near, :], x_ref[far, :]], axis=0).T
            real, imag = block[:X_ROWS], block[X_ROWS:]
            if comp == COMPS - 1:
                real, imag = -imag, real
            if k == 0:
                nyquist = imag[:, :1]
                put(middle, jnp.where(lane < half, 0.0, real), jnp.where(lane < half, 0.0, imag))
                scale = jnp.where(lane < half, jnp.where(lane == 0, 0.5, 1.0), 0.0)
                real, imag = real * scale, imag * scale
            put(k, real, imag)
        columns.append(nyquist)
    lines_ref[...] = triple_dot(high_ref[...], low_ref[...], table_ref)
    for comp in range(COMPS):
        base = comp * (middle + 1) * X_ROWS
        nyquist = columns[comp]
        for g in range(X_ROWS // group):
            cos_in = [None] * (middle + 1)
            sin_in = [None] * (middle + 1)
            for k in range(middle + 1):
                rows = slice(base + k * X_ROWS + g * group, base + k * X_ROWS + (g + 1) * group)
                real = lines_ref[rows, :LANES]
                if k == 0:
                    cos_in[0] = 2.0 * real + nyquist[g * group : (g + 1) * group] * alternate
                    continue
                imag = lines_ref[rows, LANES:]
                cosine = twiddle_ref[2 * k - 2 : 2 * k - 1, :]
                sine = twiddle_ref[2 * k - 1 : 2 * k, :]
                cos_in[k] = real * cosine - imag * sine
                if k < middle:
                    sin_in[k] = -(real * sine + imag * cosine)
            values = real_sum(cos_in, sin_in, COARSE)
            top = comp * X_ROWS + g * group
            for a in range(COARSE):
                result_ref[top : top + group, FINE * a : FINE * (a + 1)] = values[a]
        span = pl.ds(comp * X_ROWS, X_ROWS)
        copy = pltpu.make_async_copy(result_ref.at[span], out_hbm.at[span], sem.at[comp])
        copy.start()
        copies.append(copy)
    for copy in copies:
        copy.wait()


VMEM = pl.BlockSpec(memory_space=pltpu.VMEM)
HBM = pl.BlockSpec(memory_space=pltpu.HBM)
FINE_ROWS = COMPS * (COARSE // 2 + 1) * X_ROWS


def params(mebibytes):
    return pltpu.CompilerParams(vmem_limit_bytes=mebibytes * 1024 * 1024)


def edge_lines(kernel):
    return pl.pallas_call(
        edge_kernel,
        in_specs=[HBM],
        out_specs=VMEM,
        out_shape=jax.ShapeDtypeStruct((EDGES, CELLS), F32),
        scratch_shapes=[
            pltpu.VMEM((CELLS // LANES, OFFSETS, EDGE_PARTS, 1, LANES), F32),
            pltpu.SemaphoreType.DMA((CELLS // LANES, 2)),
        ],
        compiler_params=params(58),
        name="edge_lines",
    )(kernel)


def forward_y(field):
    table = stacked(fine_table())
    twiddle = y_twiddle(-1.0, 1.0)
    return pl.pallas_call(
        forward_y_kernel,
        in_specs=[VMEM] * 3,
        out_specs=HBM,
        out_shape=jax.ShapeDtypeStruct((DEVICES, SLOT, LANES), F32),
        scratch_shapes=[
            pltpu.VMEM((FINE_ROWS, 2 * LANES), BF16),
            pltpu.VMEM((FINE_ROWS, 2 * LANES), BF16),
            pltpu.VMEM((DEVICES * SLOT, LANES), F32),
            pltpu.SemaphoreType.DMA((COMPS,)),
        ],
        compiler_params=params(48),
        name="forward_y",
    )(field, jnp.asarray(table), jnp.asarray(twiddle))


def relayout(kernel, flag):
    groups = 3
    rows = OPS // groups * 16
    out_rows = OPS // groups * OWNED
    return pl.pallas_call(
        relayout_kernel,
        grid=(groups,),
        in_specs=[
            pl.BlockSpec(memory_space=pltpu.SMEM),
            pl.BlockSpec((rows, CELLS), lambda g: (g, 0)),
        ],
        out_specs=pl.BlockSpec((ROWS, out_rows, LANES), lambda g: (0, g, 0)),
        out_shape=jax.ShapeDtypeStruct((ROWS, OPS * OWNED, LANES), F32),
        scratch_shapes=[pltpu.VMEM((out_rows, CELLS), F32), pltpu.VMEM((CELLS, LANES), F32)],
        compiler_params=params(48),
        name="relayout",
    )(flag, kernel)


def spectral(lines, kernel, delta):
    twiddle = x_twiddle(-1.0, 1.0, 1.0)
    back_twiddle = x_twiddle(1.0, -1.0 / (CELLS * CELLS), -1.0)
    return pl.pallas_call(
        spectral_kernel,
        in_specs=[VMEM, HBM] + [VMEM] * 5,
        out_specs=VMEM,
        out_shape=jax.ShapeDtypeStruct((DEVICES * SLOT, LANES), F32),
        scratch_shapes=[
            pltpu.VMEM((ROWS * OPS * OWNED, LANES), F32),
            pltpu.VMEM((ROWS * EXTRA, LANES), F32),
            pltpu.VMEM((ROWS * P1_ALL, LANES), F32),
            pltpu.VMEM((ROWS * P1_ALL, 2 * LANES), BF16),
            pltpu.VMEM((ROWS * P1_ALL, LANES), F32),
            pltpu.VMEM((ROWS * P1_ROWS, LANES), F32),
            pltpu.VMEM((ROWS * P1_ROWS, LANES), F32),
            pltpu.SemaphoreType.DMA,
        ],
        compiler_params=params(48),
        name="spectral",
    )(
        lines,
        kernel,
        delta,
        jnp.asarray(twiddle),
        jnp.asarray(back_twiddle),
        jnp.asarray(x_tables(-1.0)),
        jnp.asarray(x_tables(1.0)),
    )


def inverse_y(spectra):
    rows = COMPS * X_ROWS
    return pl.pallas_call(
        inverse_y_kernel,
        in_specs=[VMEM] * 3,
        out_specs=HBM,
        out_shape=jax.ShapeDtypeStruct((rows, CELLS), F32),
        scratch_shapes=[
            pltpu.VMEM((FINE_ROWS, 2 * LANES), BF16),
            pltpu.VMEM((FINE_ROWS, 2 * LANES), BF16),
            pltpu.VMEM((FINE_ROWS, 2 * LANES), F32),
            pltpu.VMEM((rows, CELLS), F32),
            pltpu.SemaphoreType.DMA((COMPS,)),
        ],
        compiler_params=params(20),
        name="inverse_y",
    )(spectra, jnp.asarray(stacked(fine_table().T)), jnp.asarray(y_twiddle(1.0, 2.0)))


def exchange(lines):
    moved = lax.all_to_all(lines.reshape(DEVICES, SLOT, LANES), ("layer", "row"), 0, 0, tiled=True)
    return moved.reshape(DEVICES * SLOT, LANES)


def local(magnet, kernel):
    axes = ("layer", "row")
    device = lax.axis_index(axes)
    field = magnet.reshape(COMPS * X_ROWS, CELLS)
    flag = (device >= DEVICES // 2).astype(jnp.int32).reshape(1)
    edge = edge_lines(kernel)
    middle = lax.ppermute(edge, axes, [(DEVICES // 2, 0)])
    sent = forward_y(field)
    got = exchange(sent)
    coefficient = relayout(kernel.reshape(OPS * 16, CELLS), flag)
    delta = jnp.where(device == 0, middle - edge, 0.0)
    delta = jnp.swapaxes(delta.reshape(EDGES, X_ROWS, ROWS), 1, 2)
    delta = jnp.concatenate([delta, delta], axis=2).reshape(EDGES * ROWS, LANES)
    fields = spectral(got, coefficient.reshape(ROWS * OPS * OWNED, LANES), delta)
    result = inverse_y(exchange(fields))
    return result.reshape(COMPS, 1, X_ROWS, CELLS)


def solution(mesh):
    in_specs = (P(None, "layer", "row", None), P(None, None, ("layer", "row"), None))
    out_specs = P(None, "layer", "row", None)
    return jax.shard_map(local, mesh=mesh, in_specs=in_specs, out_specs=out_specs, check_vma=False)
```

profile of v0, /device:TPU:1, one launch (start us, length us, event | category | flops | bytes accessed | tf_op | source)
XLA Modules:
  0.0 78.8 jit_solution(13051917748720030969)
XLA Ops:
  0.0 1.4 %copy-done.1 = f32[3,1,64,2048]{3,2,1,0:T(8,128)S(1)} copy-done((f32[3,1,64,2048]{3,2,1,0:T(8,128)S(1)}, f32[3,1,64,2048]{3,2,1,0:T(8,128)}, u32[]{:S(2)}) %copy-start.1) | copy-done | bytes 1572888
  1.4 0.9 %copy-done.5 = bf16[512,256]{1,0:T(8,128)(2,1)S(1)} copy-done((bf16[512,256]{1,0:T(8,128)(2,1)S(1)}, bf16[512,256]{1,0:T(8,128)(2,1)}, u32[]{:S(2)}) %copy-start.5) | copy-done | bytes 262168
  2.4 0.7 copy-done.9
  3.1 2.3 %forward_y.1 = f32[128,24,128]{2,1,0:T(8,128)} custom-call(f32[192,2048]{1,0:T(8,128)S(1)} %bitcast.17, bf16[512,256]{1,0:T(8,128)(2,1)S(1)} %copy-done.5, f32[16,128]{1,0:T(8,128)S(1)} %copy-done.9), custom_call_target="tpu_custom_call" | custom-call | tf_op jit(solution)/shard_map/forward_y/pallas_call | solution.py:612
  5.4 11.5 %all-to-all-start = ((f32[128,24,128]{2,1,0:T(8,128)}), f32[128,24,128]{2,1,0:T(8,128)S(1)}, u32[]{:S(2)}, u32[]{:S(2)}) async-start(f32[128,24,128]{2,1,0:T(8,128)} %forward_y.1), calls=%async_computation | async-start | bytes 3145728 | tf_op jit(solution)/shard_map/all_to_all | solution.py:698
  16.9 2.0 %edge_lines.1 = f32[28,2048]{1,0:T(8,128)} custom-call(f32[7,6,16,2048]{3,2,1,0:T(8,128)} %kernel_hbm.1), custom_call_target="tpu_custom_call" | custom-call | tf_op jit(solution)/shard_map/edge_lines/pallas_call | solution.py:595
  18.9 0.7 collective-permute-start
  19.6 6.8 %relayout.1 = f32[32,336,128]{2,1,0:T(8,128)S(1)} custom-call(s32[1]{0:T(128)} %bitcast.2.flag_ref, f32[672,2048]{1,0:T(8,128)} %bitcast.18), custom_call_target="tpu_custom_call" | custom-call | tf_op jit(solution)/shard_map/relayout/pallas_call | solution.py:632
  26.4 2.4 %copy-done = f32[32,336,128]{2,1,0:T(8,128)} copy-done((f32[32,336,128]{2,1,0:T(8,128)}, f32[32,336,128]{2,1,0:T(8,128)S(1)}, u32[]{:S(2)}) %copy-start) | copy-done | bytes 5505048
  28.8 0.0 collective-permute-done
  28.9 0.0 copy-start.2
  28.9 0.0 copy-start.3
  28.9 0.0 copy-start.6
  28.9 0.0 copy-start.7
  28.9 0.3 reshape.38
  29.2 0.3 copy.15
  29.5 0.2 pad_maximum_fusion
  29.7 12.1 %all-to-all-done = f32[128,24,128]{2,1,0:T(8,128)S(1)} async-done(((f32[128,24,128]{2,1,0:T(8,128)}), f32[128,24,128]{2,1,0:T(8,128)S(1)}, u32[]{:S(2)}, u32[]{:S(2)}) %all-to-all-start) | async-done | bytes 1572896 | tf_op jit(solution)/shard_map/all_to_all | solution.py:698
  41.9 0.0 copy-done.6
  41.9 5.4 %spectral.1 = f32[3072,128]{1,0:T(8,128)S(1)} custom-call(f32[3072,128]{1,0:T(8,128)S(1)} %bitcast.14, f32[10752,128]{1,0:T(8,128)} %bitcast.12, f32[896,128]{1,0:T(8,128)S(1)} %bitcast.16, f32[68,128]{1,0:T(8,128)S(1)} %copy-done.7, f32[68,128]{1,0:T(8,128)S(1)} %copy-done.6, bf16[512,256]{1,0:T(8,128)(2,1)S(1)} %copy-done.3, bf16[512,256]{1,0:T(8,128)(2,1)S(1)} %copy-done.2), custom_call_target="tpu_custom_call" | custom-call | tf_op jit(solution)/shard_map/spectral/pallas_call | solution.py:650
  47.3 0.0 copy-start.4
  47.3 0.0 copy-start.8
  47.3 29.5 %all_to_all.10 = f32[128,24,128]{2,1,0:T(8,128)S(1)} all-to-all(f32[128,24,128]{2,1,0:T(8,128)S(1)} %bitcast.15), channel_id=1, replica_groups=mesh['layer'=4,'row'=32] {'layer','row'}, dimensions={0} | all-to-all | bytes 3145728 | tf_op jit(solution)/shard_map/all_to_all | solution.py:698
  76.8 2.0 %inverse_y.1 = f32[192,2048]{1,0:T(8,128)} custom-call(f32[3072,128]{1,0:T(8,128)S(1)} %bitcast.13, bf16[512,256]{1,0:T(8,128)(2,1)S(1)} %copy-done.4, f32[16,128]{1,0:T(8,128)S(1)} %copy-done.8), custom_call_target="tpu_custom_call" | custom-call | tf_op jit(solution)/shard_map/inverse_y/pallas_call | solution.py:680
  (12 shorter events, 0.1 us)
Async XLA Ops:
  0.0 1.4 %copy-start.1 = (f32[3,1,64,2048]{3,2,1,0:T(8,128)S(1)}, f32[3,1,64,2048]{3,2,1,0:T(8,128)}, u32[]{:S(2)}) copy-start(f32[3,1,64,2048]{3,2,1,0:T(8,128)} %param.10) | copy-start | bytes 4718596
  1.4 0.9 %copy-start.5 = (bf16[512,256]{1,0:T(8,128)(2,1)S(1)}, bf16[512,256]{1,0:T(8,128)(2,1)}, u32[]{:S(2)}) copy-start(bf16[512,256]{1,0:T(8,128)(2,1)} %constant.33.clone.table_ref) | copy-start | bytes 786436
  2.4 0.7 copy-start.9
  5.4 36.5 %all-to-all-start = ((f32[128,24,128]{2,1,0:T(8,128)}), f32[128,24,128]{2,1,0:T(8,128)S(1)}, u32[]{:S(2)}, u32[]{:S(2)}) async-start(f32[128,24,128]{2,1,0:T(8,128)} %forward_y.1), calls=%async_computation | async-start | bytes 3145728 | tf_op jit(solution)/shard_map/all_to_all | solution.py:698
  18.9 10.0 %collective-permute-start = (f32[28,2048]{1,0:T(8,128)}, f32[28,2048]{1,0:T(8,128)S(1)}, u32[]{:S(2)}, u32[]{:S(2)}) collective-permute-start(f32[28,2048]{1,0:T(8,128)} %edge_lines.1), channel_id=1, source_target_pairs={{64,0}} | collective-permute-start | bytes 688136 | tf_op jit(solution)/shard_map/ppermute | solution.py:708
  19.5 9.3 %copy-start.10 = (f32[28,2048]{1,0:T(8,128)S(1)}, f32[28,2048]{1,0:T(8,128)}, u32[]{:S(2)}) copy-start(f32[28,2048]{1,0:T(8,128)} %edge_lines.1) | copy-start | bytes 688132
  26.4 2.4 %copy-start = (f32[32,336,128]{2,1,0:T(8,128)}, f32[32,336,128]{2,1,0:T(8,128)S(1)}, u32[]{:S(2)}) copy-start(f32[32,336,128]{2,1,0:T(8,128)S(1)} %relayout.1) | copy-start | bytes 16515076
  28.9 13.0 %copy-start.2 = (bf16[512,256]{1,0:T(8,128)(2,1)S(1)}, bf16[512,256]{1,0:T(8,128)(2,1)}, u32[]{:S(2)}) copy-start(bf16[512,256]{1,0:T(8,128)(2,1)} %constant.38.clone.back_table_ref) | copy-start | bytes 786436
  28.9 13.0 %copy-start.3 = (bf16[512,256]{1,0:T(8,128)(2,1)S(1)}, bf16[512,256]{1,0:T(8,128)(2,1)}, u32[]{:S(2)}) copy-start(bf16[512,256]{1,0:T(8,128)(2,1)} %constant.37.clone.table_ref) | copy-start | bytes 786436
  28.9 13.0 %copy-start.6 = (f32[68,128]{1,0:T(8,128)S(1)}, f32[68,128]{1,0:T(8,128)}, u32[]{:S(2)}) copy-start(f32[68,128]{1,0:T(8,128)} %constant.36.clone.back_twiddle_ref) | copy-start | bytes 104452
  28.9 13.0 %copy-start.7 = (f32[68,128]{1,0:T(8,128)S(1)}, f32[68,128]{1,0:T(8,128)}, u32[]{:S(2)}) copy-start(f32[68,128]{1,0:T(8,128)} %constant.35.clone.twiddle_ref) | copy-start | bytes 104452
  47.3 29.6 %copy-start.4 = (bf16[512,256]{1,0:T(8,128)(2,1)S(1)}, bf16[512,256]{1,0:T(8,128)(2,1)}, u32[]{:S(2)}) copy-start(bf16[512,256]{1,0:T(8,128)(2,1)} %constant.39.clone.table_ref) | copy-start | bytes 786436
  47.3 29.5 %copy-start.8 = (f32[16,128]{1,0:T(8,128)S(1)}, f32[16,128]{1,0:T(8,128)}, u32[]{:S(2)}) copy-start(f32[16,128]{1,0:T(8,128)} %constant.40.clone.twiddle_ref) | copy-start | bytes 24580
where the time goes:
time: 79.2 us; the launch traced here: 78.8 us
  blocking collectives  29.5 us (37%)
  Pallas kernels  18.5 us (23%)
  starting transfers between devices  12.2 us (15%)
  waiting for transfers between devices  12.1 us (15%)
  local copies, waits for them, and re-layouts  6.09 us (8%)
    all_to_all x1, blocking collectives, exchange(): lax.all_to_all(lines.reshape(DEVICES, SLOT, LANES), ('layer', 'row'), 0,...  29.5 us
    all_to_all x1, waiting for transfers between devices, exchange(): lax.all_to_all(lines.reshape(DEVICES, SLOT, LANES), ('layer', 'row'), 0,...  12.1 us
    all_to_all x1, starting transfers between devices, exchange(): lax.all_to_all(lines.reshape(DEVICES, SLOT, LANES), ('layer', 'row'), 0,...  11.5 us
    pallas_call x1, Pallas kernels, relayout(): pl.pallas_call(relayout_kernel, grid=(groups,), in_specs=[pl.BlockSpec(me...  6.85 us
    unnamed x22, local copies, waits for them, and re-layouts  5.5 us
    pallas_call x1, Pallas kernels, spectral(): pl.pallas_call(spectral_kernel, in_specs=[VMEM, HBM] + [VMEM] * 5, out_sp...  5.37 us
    pallas_call x1, Pallas kernels, forward_y(): pl.pallas_call(forward_y_kernel, in_specs=[VMEM] * 3, out_specs=HBM, out_...  2.33 us
    pallas_call x1, Pallas kernels, inverse_y(): pl.pallas_call(inverse_y_kernel, in_specs=[VMEM] * 3, out_specs=HBM, out_...  1.98 us
  transfers between devices with their start and end apart: 2, of which 1 were waited for; matrix products, arithmetic and copies ran while one was open for 1% of the time, Pallas kernels for 11%

commit v1 on v0

--- a/solution.py
+++ b/solution.py
@@ -311,8 +311,16 @@
     back_ref,
     kernel_sem,
 ):
-    fetch = pltpu.make_async_copy(kernel_hbm, kernel_ref, kernel_sem)
-    fetch.start()
+    span = 8
+    piece = span * OPS * OWNED
+
+    def fetch(step):
+        start = step * piece if isinstance(step, int) else pl.multiple_of(step * piece, OWNED)
+        rows = pl.ds(start, piece)
+        return pltpu.make_async_copy(kernel_hbm.at[rows], kernel_ref.at[rows], kernel_sem.at[step])
+
+    for step in range(ROWS // span):
+        fetch(step).start()
     half = ROWS // 2
     lane = lax.broadcasted_iota(jnp.int32, (ROWS, LANES), 1)
 
@@ -398,7 +406,6 @@
         twist(k)
     forward_dot(11, 5, 0)
     forward_dot(half, 6, 1)
-    fetch.wait()
 
     def mix(spectra, coefficient, edge=False):
         fields = []
@@ -468,11 +475,12 @@
         both = dot(pair_ref[pl.ds(p1 * P1_ROWS, rows), :], back_table_ref[pl.ds(base, size), :])
         back_ref[pl.ds(p1 * P1_ROWS, rows), :] = both[:, :LANES] + both[:, LANES:]
 
-    span = 8
+    fetch(0).wait()
     for p1 in range(span):
         mix_line(p1)
 
     def mix_step(step, carry):
+        fetch(step).wait()
         p1 = pl.multiple_of(span * step, span)
         backward_dot(p1 - span, span * P1_ROWS)
         for i in range(span):
@@ -660,7 +668,7 @@
             pltpu.VMEM((ROWS * P1_ALL, LANES), F32),
             pltpu.VMEM((ROWS * P1_ROWS, LANES), F32),
             pltpu.VMEM((ROWS * P1_ROWS, LANES), F32),
-            pltpu.SemaphoreType.DMA,
+            pltpu.SemaphoreType.DMA((4,)),
         ],
         compiler_params=params(48),
         name="spectral",

time: 79.2 us -> 78.3 us (0.989)
  Pallas kernels: 18.5 us -> 17.6 us
    pallas_call x1, Pallas kernels: 5.37 us -> 4.5 us  [spectral(): pl.pallas_call(spectral_kernel, in_specs=[VMEM, HBM] + [VMEM] * 5, out_sp...]
where the time goes in v1:
time: 78.3 us; the launch traced here: 77.9 us
  blocking collectives  29.5 us (38%)
  Pallas kernels  17.6 us (22%)
  starting transfers between devices  12.2 us (16%)
  waiting for transfers between devices  12.1 us (15%)
  local copies, waits for them, and re-layouts  6.09 us (8%)
    all_to_all x1, blocking collectives, exchange(): lax.all_to_all(lines.reshape(DEVICES, SLOT, LANES), ('layer', 'row'), 0,...  29.5 us
    all_to_all x1, waiting for transfers between devices, exchange(): lax.all_to_all(lines.reshape(DEVICES, SLOT, LANES), ('layer', 'row'), 0,...  12.1 us
    all_to_all x1, starting transfers between devices, exchange(): lax.all_to_all(lines.reshape(DEVICES, SLOT, LANES), ('layer', 'row'), 0,...  11.5 us
    pallas_call x1, Pallas kernels, relayout(): pl.pallas_call(relayout_kernel, grid=(groups,), in_specs=[pl.BlockSpec(me...  6.85 us
    unnamed x22, local copies, waits for them, and re-layouts  5.5 us
    pallas_call x1, Pallas kernels, spectral(): pl.pallas_call(spectral_kernel, in_specs=[VMEM, HBM] + [VMEM] * 5, out_sp...  4.5 us
    pallas_call x1, Pallas kernels, forward_y(): pl.pallas_call(forward_y_kernel, in_specs=[VMEM] * 3, out_specs=HBM, out_...  2.33 us
    pallas_call x1, Pallas kernels, inverse_y(): pl.pallas_call(inverse_y_kernel, in_specs=[VMEM] * 3, out_specs=HBM, out_...  1.98 us
  transfers between devices with their start and end apart: 2, of which 1 were waited for; matrix products, arithmetic and copies ran while one was open for 1% of the time, Pallas kernels for 11%

profile of v1, /device:TPU:1, one launch (start us, length us, event | category | flops | bytes accessed | tf_op | source)
XLA Modules:
  0.0 77.9 jit_solution(7868074045945402642)
XLA Ops:
  0.0 1.4 %copy-done.1 = f32[3,1,64,2048]{3,2,1,0:T(8,128)S(1)} copy-done((f32[3,1,64,2048]{3,2,1,0:T(8,128)S(1)}, f32[3,1,64,2048]{3,2,1,0:T(8,128)}, u32[]{:S(2)}) %copy-start.1) | copy-done | bytes 1572888
  1.4 0.9 %copy-done.5 = bf16[512,256]{1,0:T(8,128)(2,1)S(1)} copy-done((bf16[512,256]{1,0:T(8,128)(2,1)S(1)}, bf16[512,256]{1,0:T(8,128)(2,1)}, u32[]{:S(2)}) %copy-start.5) | copy-done | bytes 262168
  2.4 0.7 copy-done.9
  3.1 2.3 %forward_y.1 = f32[128,24,128]{2,1,0:T(8,128)} custom-call(f32[192,2048]{1,0:T(8,128)S(1)} %bitcast.17, bf16[512,256]{1,0:T(8,128)(2,1)S(1)} %copy-done.5, f32[16,128]{1,0:T(8,128)S(1)} %copy-done.9), custom_call_target="tpu_custom_call" | custom-call | tf_op jit(solution)/shard_map/forward_y/pallas_call | solution.py:620
  5.4 11.5 %all-to-all-start = ((f32[128,24,128]{2,1,0:T(8,128)}), f32[128,24,128]{2,1,0:T(8,128)S(1)}, u32[]{:S(2)}, u32[]{:S(2)}) async-start(f32[128,24,128]{2,1,0:T(8,128)} %forward_y.1), calls=%async_computation | async-start | bytes 3145728 | tf_op jit(solution)/shard_map/all_to_all | solution.py:706
  16.9 2.0 %edge_lines.1 = f32[28,2048]{1,0:T(8,128)} custom-call(f32[7,6,16,2048]{3,2,1,0:T(8,128)} %kernel_hbm.1), custom_call_target="tpu_custom_call" | custom-call | tf_op jit(solution)/shard_map/edge_lines/pallas_call | solution.py:603
  18.9 0.7 collective-permute-start
  19.6 6.8 %relayout.1 = f32[32,336,128]{2,1,0:T(8,128)S(1)} custom-call(s32[1]{0:T(128)} %bitcast.2.flag_ref, f32[672,2048]{1,0:T(8,128)} %bitcast.18), custom_call_target="tpu_custom_call" | custom-call | tf_op jit(solution)/shard_map/relayout/pallas_call | solution.py:640
  26.4 2.4 %copy-done = f32[32,336,128]{2,1,0:T(8,128)} copy-done((f32[32,336,128]{2,1,0:T(8,128)}, f32[32,336,128]{2,1,0:T(8,128)S(1)}, u32[]{:S(2)}) %copy-start) | copy-done | bytes 5505048
  28.8 0.0 collective-permute-done
  28.9 0.0 copy-start.2
  28.9 0.0 copy-start.3
  28.9 0.0 copy-start.6
  28.9 0.0 copy-start.7
  28.9 0.3 reshape.38
  29.2 0.3 copy.15
  29.5 0.2 pad_maximum_fusion
  29.7 12.1 %all-to-all-done = f32[128,24,128]{2,1,0:T(8,128)S(1)} async-done(((f32[128,24,128]{2,1,0:T(8,128)}), f32[128,24,128]{2,1,0:T(8,128)S(1)}, u32[]{:S(2)}, u32[]{:S(2)}) %all-to-all-start) | async-done | bytes 1572896 | tf_op jit(solution)/shard_map/all_to_all | solution.py:706
  41.9 0.0 copy-done.6
  41.9 4.5 %spectral.1 = f32[3072,128]{1,0:T(8,128)S(1)} custom-call(f32[3072,128]{1,0:T(8,128)S(1)} %bitcast.14, f32[10752,128]{1,0:T(8,128)} %bitcast.12, f32[896,128]{1,0:T(8,128)S(1)} %bitcast.16, f32[68,128]{1,0:T(8,128)S(1)} %copy-done.7, f32[68,128]{1,0:T(8,128)S(1)} %copy-done.6, bf16[512,256]{1,0:T(8,128)(2,1)S(1)} %copy-done.3, bf16[512,256]{1,0:T(8,128)(2,1)S(1)} %copy-done.2), custom_call_target="tpu_custom_call" | custom-call | tf_op jit(solution)/shard_map/spectral/pallas_call | solution.py:658
  46.4 0.0 copy-start.4
  46.4 0.0 copy-start.8
  46.4 29.5 %all_to_all.10 = f32[128,24,128]{2,1,0:T(8,128)S(1)} all-to-all(f32[128,24,128]{2,1,0:T(8,128)S(1)} %bitcast.15), channel_id=1, replica_groups=mesh['layer'=4,'row'=32] {'layer','row'}, dimensions={0} | all-to-all | bytes 3145728 | tf_op jit(solution)/shard_map/all_to_all | solution.py:706
  75.9 2.0 %inverse_y.1 = f32[192,2048]{1,0:T(8,128)} custom-call(f32[3072,128]{1,0:T(8,128)S(1)} %bitcast.13, bf16[512,256]{1,0:T(8,128)(2,1)S(1)} %copy-done.4, f32[16,128]{1,0:T(8,128)S(1)} %copy-done.8), custom_call_target="tpu_custom_call" | custom-call | tf_op jit(solution)/shard_map/inverse_y/pallas_call | solution.py:688
  (12 shorter events, 0.1 us)
Async XLA Ops:
  0.0 1.4 %copy-start.1 = (f32[3,1,64,2048]{3,2,1,0:T(8,128)S(1)}, f32[3,1,64,2048]{3,2,1,0:T(8,128)}, u32[]{:S(2)}) copy-start(f32[3,1,64,2048]{3,2,1,0:T(8,128)} %param.10) | copy-start | bytes 4718596
  1.4 0.9 %copy-start.5 = (bf16[512,256]{1,0:T(8,128)(2,1)S(1)}, bf16[512,256]{1,0:T(8,128)(2,1)}, u32[]{:S(2)}) copy-start(bf16[512,256]{1,0:T(8,128)(2,1)} %constant.33.clone.table_ref) | copy-start | bytes 786436
  2.4 0.7 copy-start.9
  5.4 36.5 %all-to-all-start = ((f32[128,24,128]{2,1,0:T(8,128)}), f32[128,24,128]{2,1,0:T(8,128)S(1)}, u32[]{:S(2)}, u32[]{:S(2)}) async-start(f32[128,24,128]{2,1,0:T(8,128)} %forward_y.1), calls=%async_computation | async-start | bytes 3145728 | tf_op jit(solution)/shard_map/all_to_all | solution.py:706
  18.9 10.0 %collective-permute-start = (f32[28,2048]{1,0:T(8,128)}, f32[28,2048]{1,0:T(8,128)S(1)}, u32[]{:S(2)}, u32[]{:S(2)}) collective-permute-start(f32[28,2048]{1,0:T(8,128)} %edge_lines.1), channel_id=1, source_target_pairs={{64,0}} | collective-permute-start | bytes 688136 | tf_op jit(solution)/shard_map/ppermute | solution.py:716
  19.5 9.3 %copy-start.10 = (f32[28,2048]{1,0:T(8,128)S(1)}, f32[28,2048]{1,0:T(8,128)}, u32[]{:S(2)}) copy-start(f32[28,2048]{1,0:T(8,128)} %edge_lines.1) | copy-start | bytes 688132
  26.4 2.4 %copy-start = (f32[32,336,128]{2,1,0:T(8,128)}, f32[32,336,128]{2,1,0:T(8,128)S(1)}, u32[]{:S(2)}) copy-start(f32[32,336,128]{2,1,0:T(8,128)S(1)} %relayout.1) | copy-start | bytes 16515076
  28.9 13.0 %copy-start.2 = (bf16[512,256]{1,0:T(8,128)(2,1)S(1)}, bf16[512,256]{1,0:T(8,128)(2,1)}, u32[]{:S(2)}) copy-start(bf16[512,256]{1,0:T(8,128)(2,1)} %constant.38.clone.back_table_ref) | copy-start | bytes 786436
  28.9 13.0 %copy-start.3 = (bf16[512,256]{1,0:T(8,128)(2,1)S(1)}, bf16[512,256]{1,0:T(8,128)(2,1)}, u32[]{:S(2)}) copy-start(bf16[512,256]{1,0:T(8,128)(2,1)} %constant.37.clone.table_ref) | copy-start | bytes 786436
  28.9 13.0 %copy-start.6 = (f32[68,128]{1,0:T(8,128)S(1)}, f32[68,128]{1,0:T(8,128)}, u32[]{:S(2)}) copy-start(f32[68,128]{1,0:T(8,128)} %constant.36.clone.back_twiddle_ref) | copy-start | bytes 104452
  28.9 13.0 %copy-start.7 = (f32[68,128]{1,0:T(8,128)S(1)}, f32[68,128]{1,0:T(8,128)}, u32[]{:S(2)}) copy-start(f32[68,128]{1,0:T(8,128)} %constant.35.clone.twiddle_ref) | copy-start | bytes 104452
  46.4 29.5 %copy-start.4 = (bf16[512,256]{1,0:T(8,128)(2,1)S(1)}, bf16[512,256]{1,0:T(8,128)(2,1)}, u32[]{:S(2)}) copy-start(bf16[512,256]{1,0:T(8,128)(2,1)} %constant.39.clone.table_ref) | copy-start | bytes 786436
  46.4 29.5 %copy-start.8 = (f32[16,128]{1,0:T(8,128)S(1)}, f32[16,128]{1,0:T(8,128)}, u32[]{:S(2)}) copy-start(f32[16,128]{1,0:T(8,128)} %constant.40.clone.twiddle_ref) | copy-start | bytes 24580

commit v2 on v1

--- a/solution.py
+++ b/solution.py
@@ -185,27 +185,25 @@
 EDGES = OFFSETS * EDGE_PARTS
 
 
-def edge_kernel(kernel_hbm, out_ref, tiles_ref, sem):
-    n_tiles = CELLS // LANES
-    copies = []
-    for j in range(n_tiles):
-        lanes = pl.ds(LANES * j, LANES)
-        for i, (source, target) in enumerate([((0, 3), (0, 3)), ((4, 1), (3, 1))]):
-            copy = pltpu.make_async_copy(
-                kernel_hbm.at[:, pl.ds(*source), pl.ds(0, 1), lanes],
-                tiles_ref.at[j, :, pl.ds(*target)],
-                sem.at[j, i],
-            )
-            copy.start()
-            copies.append(copy)
-    flat = tiles_ref.reshape(n_tiles * EDGES, LANES)
-    for j in range(n_tiles):
-        copies[2 * j].wait()
-        copies[2 * j + 1].wait()
-        out_ref[:, LANES * j : LANES * (j + 1)] = flat[pl.ds(j * EDGES, EDGES), :]
-
-
-def forward_y_kernel(x_ref, table_ref, twiddle_ref, out_hbm, high_ref, low_ref, out_ref, sem):
+def forward_y_kernel(
+    x_hbm, table_hbm, twiddle_hbm, kernel_hbm, out_hbm, edge_hbm,
+    high_ref, low_ref, out_ref, x_ref, table_ref, twiddle_ref, edge_ref, sem, load_sem, edge_sem,
+):
+    spans = [pl.ds(comp * X_ROWS, X_ROWS) for comp in range(COMPS)]
+    loads = [pltpu.make_async_copy(x_hbm.at[b], x_ref.at[b], load_sem.at[c]) for c, b in enumerate(spans)]
+    tables = [
+        pltpu.make_async_copy(twiddle_hbm, twiddle_ref, load_sem.at[COMPS]),
+        pltpu.make_async_copy(table_hbm, table_ref, load_sem.at[COMPS + 1]),
+    ]
+    lines = [
+        pltpu.make_async_copy(
+            kernel_hbm.at[:, pl.ds(*source), pl.ds(0, 1)], edge_ref.at[:, pl.ds(*target)], edge_sem.at[i]
+        )
+        for i, (source, target) in enumerate([((0, 3), (0, 3)), ((4, 1), (3, 1))])
+    ]
+    for copy in [loads[0]] + tables + loads[1:] + lines:
+        copy.start()
+    tables[0].wait()
     slots = out_ref.reshape(DEVICES, SLOT, LANES)
     saves = []
     edges = []
@@ -217,6 +215,7 @@
     for comp in range(COMPS):
         base = comp * (middle + 1) * X_ROWS
         nyquist = []
+        loads[comp].wait()
         for g in range(X_ROWS // group):
             top = comp * X_ROWS + g * group
             parts = [x_ref[top : top + group, FINE * a : FINE * (a + 1)] for a in range(COARSE)]
@@ -240,6 +239,12 @@
                 else:
                     high_ref[rows, LANES:], low_ref[rows, LANES:] = split_pair(imag)
         edges.append(jnp.concatenate(nyquist, axis=0))
+    for copy in lines:
+        copy.wait()
+    save = pltpu.make_async_copy(edge_ref, edge_hbm, edge_sem.at[2])
+    save.start()
+    saves.append(save)
+    tables[1].wait()
     out = triple_dot(high_ref[...], low_ref[...], table_ref)
     for comp in range(COMPS):
 
@@ -263,8 +268,8 @@
                 far = slot_rows(comp, middle)[1]
             out_ref[near, :] = block[:half]
             out_ref[far, :] = block[half:]
-        lines = (slice(None), pl.ds(comp * OWNED, OWNED))
-        save = pltpu.make_async_copy(slots.at[lines], out_hbm.at[lines], sem.at[comp])
+        part = (slice(None), pl.ds(comp * OWNED, OWNED))
+        save = pltpu.make_async_copy(slots.at[part], out_hbm.at[part], sem.at[comp])
         save.start()
         saves.append(save)
     for save in saves:
@@ -599,38 +604,30 @@
     return pltpu.CompilerParams(vmem_limit_bytes=mebibytes * 1024 * 1024)
 
 
-def edge_lines(kernel):
-    return pl.pallas_call(
-        edge_kernel,
-        in_specs=[HBM],
-        out_specs=VMEM,
-        out_shape=jax.ShapeDtypeStruct((EDGES, CELLS), F32),
-        scratch_shapes=[
-            pltpu.VMEM((CELLS // LANES, OFFSETS, EDGE_PARTS, 1, LANES), F32),
-            pltpu.SemaphoreType.DMA((CELLS // LANES, 2)),
-        ],
-        compiler_params=params(58),
-        name="edge_lines",
-    )(kernel)
-
-
-def forward_y(field):
+def forward_y(field, kernel):
     table = stacked(fine_table())
     twiddle = y_twiddle(-1.0, 1.0)
+    edge = (OFFSETS, EDGE_PARTS, 1, CELLS)
     return pl.pallas_call(
         forward_y_kernel,
-        in_specs=[VMEM] * 3,
-        out_specs=HBM,
-        out_shape=jax.ShapeDtypeStruct((DEVICES, SLOT, LANES), F32),
+        in_specs=[HBM] * 4,
+        out_specs=[HBM, HBM],
+        out_shape=[jax.ShapeDtypeStruct((DEVICES, SLOT, LANES), F32), jax.ShapeDtypeStruct(edge, F32)],
         scratch_shapes=[
             pltpu.VMEM((FINE_ROWS, 2 * LANES), BF16),
             pltpu.VMEM((FINE_ROWS, 2 * LANES), BF16),
             pltpu.VMEM((DEVICES * SLOT, LANES), F32),
+            pltpu.VMEM((COMPS * X_ROWS, CELLS), F32),
+            pltpu.VMEM(table.shape, BF16),
+            pltpu.VMEM(twiddle.shape, F32),
+            pltpu.VMEM(edge, F32),
             pltpu.SemaphoreType.DMA((COMPS,)),
+            pltpu.SemaphoreType.DMA((COMPS + 2,)),
+            pltpu.SemaphoreType.DMA((3,)),
         ],
-        compiler_params=params(48),
+        compiler_params=params(63),
         name="forward_y",
-    )(field, jnp.asarray(table), jnp.asarray(twiddle))
+    )(field, jnp.asarray(table), jnp.asarray(twiddle), kernel)
 
 
 def relayout(kernel, flag):
@@ -712,9 +709,8 @@
     device = lax.axis_index(axes)
     field = magnet.reshape(COMPS * X_ROWS, CELLS)
     flag = (device >= DEVICES // 2).astype(jnp.int32).reshape(1)
-    edge = edge_lines(kernel)
+    sent, edge = forward_y(field, kernel)
     middle = lax.ppermute(edge, axes, [(DEVICES // 2, 0)])
-    sent = forward_y(field)
     got = exchange(sent)
     coefficient = relayout(kernel.reshape(OPS * 16, CELLS), flag)
     delta = jnp.where(device == 0, middle - edge, 0.0)

time: 78.3 us -> 77.9 us (level)
  local copies, waits for them, and re-layouts: 6.09 us -> 3.85 us
  other arithmetic: 0.23 us -> 2.18 us
  blocking collectives: 29.5 us -> 30.9 us
    unnamed x22 -> x16, local copies, waits for them, and re-layouts: 5.5 us -> 2.46 us
    all_to_all x1, blocking collectives: 29.5 us -> 30.9 us  [exchange(): lax.all_to_all(lines.reshape(DEVICES, SLOT, LANES), ('layer', 'row'), 0,...]
    concatenate x1, other arithmetic: 0.19 us -> 1.34 us  [local(): delta = jnp.concatenate([delta, delta], axis=2).reshape(EDGES * ROWS, LANES)]
    select_n x1, other arithmetic: 0.04 us -> 0.84 us  [local(): delta = jnp.where(device == 0, middle - edge, 0.0)]
    transpose x1, local copies, waits for them, and re-layouts: 0.29 us -> 1.08 us  [local(): delta = jnp.swapaxes(delta.reshape(EDGES, X_ROWS, ROWS), 1, 2)]
    pallas_call x2 -> x1, Pallas kernels: 4.28 us -> 3.7 us  [forward_y(): pl.pallas_call(forward_y_kernel, in_specs=[HBM] * 4, out_specs=[HBM, HBM]...]
  transfers between devices with their start and end apart: 2 -> 2, of which waited for: 1 -> 1; matrix products, arithmetic and copies ran while one was open for 1% -> 5% of each run, Pallas kernels for 11% -> 9%
where the time goes in v2:
time: 77.9 us; the launch traced here: 77.6 us
  blocking collectives  30.9 us (40%)
  Pallas kernels  17 us (22%)
  starting transfers between devices  12.2 us (16%)
  waiting for transfers between devices  11.4 us (15%)
  local copies, waits for them, and re-layouts  3.85 us (5%)
  other arithmetic  2.18 us (3%)
    all_to_all x1, blocking collectives, exchange(): lax.all_to_all(lines.reshape(DEVICES, SLOT, LANES), ('layer', 'row'), 0,...  30.9 us
    all_to_all x1, starting transfers between devices, exchange(): lax.all_to_all(lines.reshape(DEVICES, SLOT, LANES), ('layer', 'row'), 0,...  11.5 us
    all_to_all x1, waiting for transfers between devices, exchange(): lax.all_to_all(lines.reshape(DEVICES, SLOT, LANES), ('layer', 'row'), 0,...  11.4 us
    pallas_call x1, Pallas kernels, relayout(): pl.pallas_call(relayout_kernel, grid=(groups,), in_specs=[pl.BlockSpec(me...  6.81 us
    pallas_call x1, Pallas kernels, spectral(): pl.pallas_call(spectral_kernel, in_specs=[VMEM, HBM] + [VMEM] * 5, out_sp...  4.49 us
    pallas_call x1, Pallas kernels, forward_y(): pl.pallas_call(forward_y_kernel, in_specs=[HBM] * 4, out_specs=[HBM, HBM]...  3.7 us
    unnamed x16, local copies, waits for them, and re-layouts  2.46 us
    pallas_call x1, Pallas kernels, inverse_y(): pl.pallas_call(inverse_y_kernel, in_specs=[VMEM] * 3, out_specs=HBM, out_...  1.98 us
  transfers between devices with their start and end apart: 2, of which 1 were waited for; matrix products, arithmetic and copies ran while one was open for 5% of the time, Pallas kernels for 9%

profile of v2, /device:TPU:1, one launch (start us, length us, event | category | flops | bytes accessed | tf_op | source)
XLA Modules:
  0.0 77.6 jit_solution(315027491756200989)
XLA Ops:
  0.0 3.7 %forward_y.1 = (f32[128,24,128]{2,1,0:T(8,128)}, f32[7,4,1,2048]{3,2,1,0:T(1,128)}) custom-call(f32[192,2048]{1,0:T(8,128)} %bitcast.19, bf16[512,256]{1,0:T(8,128)(2,1)} %constant.33.clone.table_hbm, f32[16,128]{1,0:T(8,128)} %constant.34.clone.twiddle_hbm, f32[7,6,16,2048]{3,2,1,0:T(8,128)} %kernel_hbm.1), custom_call_target="tpu_custom_call" | custom-call | tf_op jit(solution)/shard_map/forward_y/pallas_call | solution.py:611
  3.7 0.0 copy-start.7
  3.7 11.5 %all-to-all-start = ((f32[128,24,128]{2,1,0:T(8,128)}), f32[128,24,128]{2,1,0:T(8,128)S(1)}, u32[]{:S(2)}, u32[]{:S(2)}) async-start(f32[128,24,128]{2,1,0:T(8,128)} %get-tuple-element.7), calls=%async_computation | async-start | bytes 3145728 | tf_op jit(solution)/shard_map/all_to_all | solution.py:703
  15.2 0.0 copy-done.7
  15.2 0.7 collective-permute-start
  15.9 6.8 %relayout.1 = f32[32,336,128]{2,1,0:T(8,128)S(1)} custom-call(s32[1]{0:T(128)} %bitcast.2.flag_ref, f32[672,2048]{1,0:T(8,128)} %bitcast.17), custom_call_target="tpu_custom_call" | custom-call | tf_op jit(solution)/shard_map/relayout/pallas_call | solution.py:637
  22.7 0.0 copy-start
  22.7 2.4 %copy-done = f32[32,336,128]{2,1,0:T(8,128)} copy-done((f32[32,336,128]{2,1,0:T(8,128)}, f32[32,336,128]{2,1,0:T(8,128)S(1)}, u32[]{:S(2)}) %copy-start) | copy-done | bytes 5505048
  25.2 0.0 collective-permute-done
  25.2 0.8 %fusion = f32[7,4,2048]{2,1,0:T(4,128)S(1)} fusion(pred[]{:T(512)S(6)} %eq.3, f32[7,4,1,2048]{3,2,1,0:T(1,128)S(1)} %collective-permute-done, f32[7,4,1,2048]{3,2,1,0:T(1,128)S(1)} %copy-done.7), kind=kLoop, calls=%fused_computation.2 | loop fusion | flops 114688 | bytes 688129 | tf_op jit(solution)/shard_map/jit(_where)/select_n | solution.py:716
  26.0 0.0 copy-start.1
  26.0 0.0 copy-start.2
  26.0 0.0 copy-start.4
  26.0 0.0 copy-start.5
  26.1 0.3 reshape.38
  26.4 1.1 %copy.15 = f32[28,32,64]{2,1,0:T(8,128)} copy(f32[28,32,64]{1,2,0:T(8,128)S(1)} %bitcast.18) | data formatting | bytes 458752 | tf_op jit(solution)/shard_map/transpose | solution.py:717
  27.5 1.3 %pad_maximum_fusion = f32[28,32,128]{2,1,0:T(8,128)S(1)} fusion(f32[28,32,64]{2,1,0:T(8,128)} %copy.15), kind=kLoop, calls=%fused_computation | loop fusion | flops 114688 | bytes 688128 | tf_op jit(solution)/shard_map/concatenate | solution.py:718
  28.8 11.4 %all-to-all-done = f32[128,24,128]{2,1,0:T(8,128)S(1)} async-done(((f32[128,24,128]{2,1,0:T(8,128)}), f32[128,24,128]{2,1,0:T(8,128)S(1)}, u32[]{:S(2)}, u32[]{:S(2)}) %all-to-all-start) | async-done | bytes 1572896 | tf_op jit(solution)/shard_map/all_to_all | solution.py:703
  40.2 0.0 copy-done.4
  40.2 4.5 %spectral.1 = f32[3072,128]{1,0:T(8,128)S(1)} custom-call(f32[3072,128]{1,0:T(8,128)S(1)} %bitcast.14, f32[10752,128]{1,0:T(8,128)} %bitcast.12, f32[896,128]{1,0:T(8,128)S(1)} %bitcast.16, f32[68,128]{1,0:T(8,128)S(1)} %copy-done.5, f32[68,128]{1,0:T(8,128)S(1)} %copy-done.4, bf16[512,256]{1,0:T(8,128)(2,1)S(1)} %copy-done.2, bf16[512,256]{1,0:T(8,128)(2,1)S(1)} %copy-done.1), custom_call_target="tpu_custom_call" | custom-call | tf_op jit(solution)/shard_map/spectral/pallas_call | solution.py:655
  44.7 0.0 copy-start.3
  44.7 0.0 copy-start.6
  44.7 30.9 %all_to_all.10 = f32[128,24,128]{2,1,0:T(8,128)S(1)} all-to-all(f32[128,24,128]{2,1,0:T(8,128)S(1)} %bitcast.15), channel_id=1, replica_groups=mesh['layer'=4,'row'=32] {'layer','row'}, dimensions={0} | all-to-all | bytes 3145728 | tf_op jit(solution)/shard_map/all_to_all | solution.py:703
  75.7 2.0 %inverse_y.1 = f32[192,2048]{1,0:T(8,128)} custom-call(f32[3072,128]{1,0:T(8,128)S(1)} %bitcast.13, bf16[512,256]{1,0:T(8,128)(2,1)S(1)} %copy-done.3, f32[16,128]{1,0:T(8,128)S(1)} %copy-done.6), custom_call_target="tpu_custom_call" | custom-call | tf_op jit(solution)/shard_map/inverse_y/pallas_call | solution.py:685
  (5 shorter events, 0.0 us)
Async XLA Ops:
  3.7 11.5 %copy-start.7 = (f32[7,4,1,2048]{3,2,1,0:T(1,128)S(1)}, f32[7,4,1,2048]{3,2,1,0:T(1,128)}, u32[]{:S(2)}) copy-start(f32[7,4,1,2048]{3,2,1,0:T(1,128)} %get-tuple-element.8) | copy-start | bytes 688132
  3.7 36.5 %all-to-all-start = ((f32[128,24,128]{2,1,0:T(8,128)}), f32[128,24,128]{2,1,0:T(8,128)S(1)}, u32[]{:S(2)}, u32[]{:S(2)}) async-start(f32[128,24,128]{2,1,0:T(8,128)} %get-tuple-element.7), calls=%async_computation | async-start | bytes 3145728 | tf_op jit(solution)/shard_map/all_to_all | solution.py:703
  15.2 9.9 %collective-permute-start = (f32[7,4,1,2048]{3,2,1,0:T(1,128)S(1)}, f32[7,4,1,2048]{3,2,1,0:T(1,128)S(1)}, u32[]{:S(2)}, u32[]{:S(2)}) collective-permute-start(f32[7,4,1,2048]{3,2,1,0:T(1,128)S(1)} %copy-done.7), channel_id=1, source_target_pairs={{64,0}} | collective-permute-start | bytes 688136 | tf_op jit(solution)/shard_map/ppermute | solution.py:713
  22.7 2.4 %copy-start = (f32[32,336,128]{2,1,0:T(8,128)}, f32[32,336,128]{2,1,0:T(8,128)S(1)}, u32[]{:S(2)}) copy-start(f32[32,336,128]{2,1,0:T(8,128)S(1)} %relayout.1) | copy-start | bytes 16515076
  26.0 14.2 %copy-start.1 = (bf16[512,256]{1,0:T(8,128)(2,1)S(1)}, bf16[512,256]{1,0:T(8,128)(2,1)}, u32[]{:S(2)}) copy-start(bf16[512,256]{1,0:T(8,128)(2,1)} %constant.38.clone.back_table_ref) | copy-start | bytes 786436
  26.0 14.2 %copy-start.2 = (bf16[512,256]{1,0:T(8,128)(2,1)S(1)}, bf16[512,256]{1,0:T(8,128)(2,1)}, u32[]{:S(2)}) copy-start(bf16[512,256]{1,0:T(8,128)(2,1)} %constant.37.clone.table_ref) | copy-start | bytes 786436
  26.0 14.2 %copy-start.4 = (f32[68,128]{1,0:T(8,128)S(1)}, f32[68,128]{1,0:T(8,128)}, u32[]{:S(2)}) copy-start(f32[68,128]{1,0:T(8,128)} %constant.36.clone.back_twiddle_ref) | copy-start | bytes 104452
  26.0 14.2 %copy-start.5 = (f32[68,128]{1,0:T(8,128)S(1)}, f32[68,128]{1,0:T(8,128)}, u32[]{:S(2)}) copy-start(f32[68,128]{1,0:T(8,128)} %constant.35.clone.twiddle_ref) | copy-start | bytes 104452
  44.7 31.0 %copy-start.3 = (bf16[512,256]{1,0:T(8,128)(2,1)S(1)}, bf16[512,256]{1,0:T(8,128)(2,1)}, u32[]{:S(2)}) copy-start(bf16[512,256]{1,0:T(8,128)(2,1)} %constant.39.clone.table_ref) | copy-start | bytes 786436
  44.7 30.9 %copy-start.6 = (f32[16,128]{1,0:T(8,128)S(1)}, f32[16,128]{1,0:T(8,128)}, u32[]{:S(2)}) copy-start(f32[16,128]{1,0:T(8,128)} %constant.40.clone.twiddle_ref) | copy-start | bytes 24580
